TPU v7x, 32 devices: a whole 2x2x4 slice. The times are simulated.
32 devices in a mesh: beam: 2 (over x), fft: 16 (over z, y, core).
Axes of the slice: x: 2, y: 2, z: 4, core: 2. Of those that a mesh axis runs over, the one named last changes fastest.
Arguments:
- baseband: bfloat16 [4, 33554432], P('beam', 'fft'), parts along dimension 0, may hold values from -6 to 6
- spectrum_in: bfloat16 [4, 4096, 8192], P('beam', 'fft'), parts along dimension 0, may hold values from -6 to 6
- dm_index: int32 [1], replicated, may hold values from 0 to 63
Outputs:
- spectrum_out: bfloat16 [4, 4096, 8192], P('beam', 'fft'), parts along dimension 0
- smoothed: float32 [2, 2097152], P('beam', 'fft'), parts along dimension 0
There are 2 independent parts, one for each index of `beam`. A program takes and returns all parts, laid end to end along the dimension named above; an argument that names none is the same for every part. Nothing has to cross between parts.
Inputs may be any that keep to these rules, and one draw needn't show every extreme that they name: `dm_index`: indices into the grid of 64 trial dispersion measures.
All inputs are finite; a program needn't handle non-finite values.
Results may differ from a plain program's by a relative error of at most 0.0019.
The roundings to bfloat16 on the way count: a program that leaves them out, or rounds other values in their place, can miss the bound.
Values may be sent and summed in bfloat16 or wider, within the bound.
A program may use at most 128 MiB of HBM per device.

v0:
```python
import math
import jax
import jax.numpy as jnp
from jax import lax
from jax.sharding import PartitionSpec as P

ROWS_OUTER = 32
ROWS_INNER = 128
COLS_OUTER = 64
COLS_INNER = 128
ROW_LENGTH = 4096
COLUMN_LENGTH = 8192
SEGMENT_SAMPLES = 33554432
DM_GRID = 64
DECIMATE_FACTOR = 16
HALF_WIDTH = 16


def padded_2(block, sides, width):
    for axis, dim in sides:
        count = lax.axis_size(axis)
        forward = [(i, i + 1) for i in range(count - 1)]
        backward = [(target, source) for source, target in forward]
        low = lax.ppermute(
            lax.slice_in_dim(block, block.shape[dim] - width, None, axis=dim), axis, forward
        )
        high = lax.ppermute(lax.slice_in_dim(block, 0, width, axis=dim), axis, backward)
        block = jnp.concatenate([low, block, high], axis=dim)
    return block


def dft_table(length, direction):
    positions = jnp.arange(length, dtype=jnp.int32)
    product = jnp.remainder(positions[:, None] * positions[None, :], length)
    radians = direction * 2.0 * math.pi / length * product.astype(jnp.float32)
    norm_scale = 1.0 / math.sqrt(length)
    cosine = jnp.cos(radians) * norm_scale
    sine_part = jnp.sin(radians) * norm_scale
    return jnp.stack([jnp.stack([cosine, sine_part]), jnp.stack([-sine_part, cosine])]).astype(
        jnp.bfloat16
    )


def radians_of(numer, modulus, direction):
    return direction * 2.0 * math.pi / modulus * jnp.remainder(numer, modulus).astype(jnp.float32)


def chirp_radians(freq_row, col_outer, col_inner, grid_steps):
    col_freq = col_outer + COLS_OUTER * col_inner
    whole_mod = 4.0 * DM_GRID * ROW_LENGTH * COLUMN_LENGTH
    cross_mod = 2 * DM_GRID * COLUMN_LENGTH
    square_mod = 4 * DM_GRID * COLUMN_LENGTH
    grid_float = grid_steps.astype(jnp.float32)
    row_square = (freq_row * freq_row).astype(jnp.float32)
    term_rows = grid_float[:, None, None, None] * row_square[None, :, None, None] / whole_mod
    cross = jnp.remainder(freq_row[:, None, None] * col_freq[None], cross_mod)
    cross = jnp.remainder(grid_steps[:, None, None, None] * cross[None], cross_mod)
    square = jnp.remainder(col_freq * col_freq, square_mod)
    square = jnp.remainder(grid_steps[:, None, None] * square[None], square_mod)
    high_part = square // 512
    low_part = square % 512
    square = jnp.remainder(
        jnp.remainder(ROW_LENGTH * high_part, square_mod) * 512 + ROW_LENGTH * low_part, square_mod
    )
    turns = (
        term_rows
        + cross.astype(jnp.float32) / cross_mod
        + square[:, None].astype(jnp.float32) / square_mod
    )
    return 2.0 * math.pi * turns


def rotate(values, radians):
    cosine = jnp.cos(radians)
    sine_part = jnp.sin(radians)
    real_part = values[:, 0] * cosine - values[:, 1] * sine_part
    imag_part = values[:, 0] * sine_part + values[:, 1] * cosine
    return jnp.stack([real_part, imag_part], axis=1).astype(jnp.bfloat16)


def dft_section(values, einsum_form, length, direction, radians):
    mixed_sum = jnp.einsum(
        einsum_form, values, dft_table(length, direction), preferred_element_type=jnp.float32
    )
    if radians is None:
        return mixed_sum.astype(jnp.bfloat16)
    return rotate(mixed_sum, radians)


def row_frequency(row_pos):
    return row_pos // ROWS_INNER + ROWS_OUTER * (row_pos % ROWS_INNER)


def chirp_front(spectrum, grid_steps, row_start, row_local):
    trial_total = grid_steps.shape[0]
    row_pos = row_start + jnp.arange(row_local, dtype=jnp.int32)
    freq_row = row_frequency(row_pos)
    col_outer = jnp.arange(COLS_OUTER, dtype=jnp.int32)[:, None]
    col_inner = jnp.arange(COLS_INNER, dtype=jnp.int32)[None, :]
    values = rotate(
        spectrum.astype(jnp.float32).reshape(1, 2, row_local, COLS_OUTER, COLS_INNER),
        chirp_radians(freq_row, col_outer, col_inner, grid_steps),
    )
    values = dft_section(
        values,
        "dimjq,ioqy->domjy",
        COLS_INNER,
        1,
        radians_of(col_outer * col_inner, COLUMN_LENGTH, 1),
    )
    col_time = COLS_INNER * col_outer + col_inner
    values = dft_section(
        values,
        "dimjy,iojx->domxy",
        COLS_OUTER,
        1,
        radians_of(freq_row[:, None, None] * col_time[None], SEGMENT_SAMPLES, 1),
    )
    return values.reshape(trial_total, 2, row_local, COLUMN_LENGTH)


def finish_rows(values):
    trial_total = values.shape[0]
    col_local = values.shape[3]
    values = values.reshape(trial_total, 2, ROWS_OUTER, ROWS_INNER, col_local)
    outer_pos = jnp.arange(ROWS_OUTER, dtype=jnp.int32)[:, None]
    inner_pos = jnp.arange(ROWS_INNER, dtype=jnp.int32)[None, :]
    values = dft_section(
        values,
        "dikqb,ioqy->dokyb",
        ROWS_INNER,
        1,
        radians_of(outer_pos * inner_pos, ROW_LENGTH, 1)[:, :, None],
    )
    values = dft_section(values, "dikyb,iokx->doxyb", ROWS_OUTER, 1, None)
    return values.reshape(trial_total, 2, ROW_LENGTH, col_local)


def detect(values):
    trial_total = values.shape[0]
    row_total = values.shape[2]
    column_total = values.shape[3]
    wide = values.astype(jnp.float32)
    detected_power = wide[:, 0] * wide[:, 0] + wide[:, 1] * wide[:, 1]
    return jnp.mean(
        detected_power.reshape(
            trial_total, row_total, column_total // DECIMATE_FACTOR, DECIMATE_FACTOR
        ),
        axis=3,
    )


def on_device(baseband, spectrum_in, dm_index):
    device_index = lax.axis_index("fft")
    row_local = spectrum_in.shape[1]
    col_local = COLUMN_LENGTH // (ROW_LENGTH // row_local)
    values = baseband.reshape(2, row_local, COLUMN_LENGTH)
    values = lax.all_to_all(values, "fft", split_axis=2, concat_axis=1, tiled=True)
    values = values.reshape(1, 2, ROWS_OUTER, ROWS_INNER, col_local)
    outer_pos = jnp.arange(ROWS_OUTER, dtype=jnp.int32)[:, None]
    inner_pos = jnp.arange(ROWS_INNER, dtype=jnp.int32)[None, :]
    values = dft_section(
        values,
        "dixyb,ioxk->dokyb",
        ROWS_OUTER,
        -1,
        radians_of(outer_pos * inner_pos, ROW_LENGTH, -1)[:, :, None],
    )
    freq_row = outer_pos + ROWS_OUTER * inner_pos
    col_pos = device_index * col_local + jnp.arange(col_local, dtype=jnp.int32)
    values = dft_section(
        values,
        "dikyb,ioyq->dokqb",
        ROWS_INNER,
        -1,
        radians_of(freq_row[:, :, None] * col_pos[None, None, :], SEGMENT_SAMPLES, -1),
    )
    values = values.reshape(1, 2, ROW_LENGTH, col_local)
    values = lax.all_to_all(values, "fft", split_axis=2, concat_axis=3, tiled=True)
    values = values.reshape(1, 2, row_local, COLS_OUTER, COLS_INNER)
    col_outer = jnp.arange(COLS_OUTER, dtype=jnp.int32)[:, None]
    col_inner = jnp.arange(COLS_INNER, dtype=jnp.int32)[None, :]
    values = dft_section(
        values,
        "dimxy,ioxj->domjy",
        COLS_OUTER,
        -1,
        radians_of(col_outer * col_inner, COLUMN_LENGTH, -1),
    )
    values = dft_section(values, "dimjy,ioyq->domjq", COLS_INNER, -1, None)
    spectrum_out = values[0].reshape(2, row_local, COLUMN_LENGTH)
    grid_steps = dm_index + 1
    row_start = device_index * row_local
    trial_total = dm_index.shape[0]
    front_part = chirp_front(spectrum_in, grid_steps, row_start, row_local)
    moved = lax.all_to_all(front_part, "fft", split_axis=3, concat_axis=2, tiled=True)
    pieces = finish_rows(moved)
    decimated_power = lax.all_to_all(
        detect(pieces).astype(jnp.bfloat16), "fft", split_axis=1, concat_axis=2, tiled=True
    ).astype(jnp.float32)
    series = decimated_power.reshape(
        trial_total, decimated_power.shape[1] * decimated_power.shape[2]
    )
    padded = padded_2(series.astype(jnp.bfloat16), (("fft", 1),), HALF_WIDTH).astype(series.dtype)
    length = series.shape[1]
    window_sum = padded[:, 0:length]
    for offset in range(1, 2 * HALF_WIDTH + 1):
        window_sum = window_sum + padded[:, offset : offset + length]
    smoothed = window_sum / (2 * HALF_WIDTH + 1)
    return (spectrum_out, smoothed)


def solution(mesh):
    placed = (P("beam", "fft"), P("beam", "fft", None), P())
    return jax.shard_map(
        on_device,
        mesh=mesh,
        in_specs=placed,
        out_specs=(P("beam", "fft", None), P("beam", "fft")),
        check_vma=False,
    )
```

profile of v0, /device:TPU:16, one launch (start us, length us, event | category | flops | bytes accessed | tf_op | source)
XLA Modules:
  0.0 1084.0 jit_solution(8108217904448306539)
XLA Ops:
  2.5 11.9 %copy.194 = bf16[2,256,8192]{1,2,0:T(8,128)(2,1)} copy(bf16[2,256,8192]{2,1,0:T(8,128)(2,1)} %param.4) | data formatting | bytes 16777216 | tf_op args[1]
  14.4 11.5 %fusion.129 = (f32[1,1,256,64,128]{2,4,3,1,0:T(8,128)}, f32[1,1,256,64,128]{2,4,3,1,0:T(8,128)}) fusion(bf16[1,2,256,64,128]{2,4,3,1,0:T(8,128)(2,1)} %bitcast.212), kind=kLoop, calls=%fused_computation.287 | loop fusion | bytes 33554432 | tf_op jit(solution)/shard_map/slice | solution.py:76
  26.0 9.0 copy.240
  35.0 9.0 copy.241
  44.0 41.0 %fusion.57 = (bf16[1,256,64,128]{3,1,0,2:T(8,128)(2,1)S(1)}, bf16[1,256,64,128]{3,1,0,2:T(8,128)(2,1)S(1)}) fusion(f32[1,1,256,64,128]{4,2,3,1,0:T(8,128)} %copy.241, f32[1,1,256,64,128]{4,2,3,1,0:T(8,128)} %copy.240, f32[64,128]{1,0:T(8,128)S(1)} %fusion.97, s32[64,128]{1,0:T(8,128)S(1)} %iota_add_fusion.1, s32[256]{0:T(256)S(1)} %fusion.122, s32[]{:T(128)} %bitcast.60, ...), kind=kLoop, calls=%fused_computation.92 | loop fusion | flops 77594624 | bytes 25233412 | tf_op jit(solution)/shard_map/stack | solution.py:78
  107.2 12.2 %copy.200 = bf16[2,256,64,128]{3,2,0,1:T(8,128)(2,1)} copy(bf16[2,256,64,128]{1,3,2,0:T(8,128)(2,1)} %pad_maximum_fusion.3) | data formatting | bytes 16777216 | tf_op jit(solution)/shard_map/stack | solution.py:78
  125.2 18.3 %copy.285 = f32[2,64,256,128]{3,2,1,0:T(8,128)S(1)} copy(f32[2,64,256,128]{3,1,2,0:T(8,128)S(1)} %fusion.48) | data formatting | bytes 33554432 | tf_op jit(solution)/shard_map/dimjy,iojx->domxy/dot_general | solution.py:82
  143.6 37.2 %subtract_convert_fusion.1 = (bf16[1,1,256,64,128]{4,2,3,1,0:T(8,128)(2,1)}, bf16[1,1,256,64,128]{4,2,3,1,0:T(8,128)(2,1)}) fusion(f32[1,2,256,64,128]{4,2,3,1,0:T(8,128)S(1)} %bitcast.213, s32[64,128]{1,0:T(8,128)S(1)} %iota_add_fusion, s32[256]{0:T(256)S(1)} %fusion.122), kind=kLoop, calls=%fused_computation.71 | loop fusion | flops 46137344 | bytes 25199616 | tf_op jit(solution)/shard_map/convert.9
  201.2 16.4 %copy.204 = bf16[1,2,256,8192]{2,1,0,3:T(2,128)(2,1)} copy(bf16[1,2,256,8192]{2,3,1,0:T(8,128)(2,1)} %pad_maximum_fusion.4) | data formatting | bytes 16777216 | tf_op jit(solution)/shard_map/stack | solution.py:78
  224.3 12.7 %copy.286 = bf16[1,2,256,8192]{3,2,1,0:T(8,128)(2,1)} copy(bf16[1,2,256,8192]{3,1,2,0:T(2,128)(2,1)} %bitcast.228) | data formatting | bytes 16777216
  237.0 21.0 %copy.183 = bf16[2,256,8192]{1,0,2:T(2,128)(2,1)} copy(bf16[2,256,8192]{2,1,0:T(8,128)(2,1)} %bitcast.222) | data formatting | bytes 16777216 | tf_op jit(solution)/shard_map/reshape | solution.py:157
  258.0 148.7 %all-to-all-done.2 = bf16[1,2,256,8192]{2,1,0,3:T(2,128)(2,1)} async-done(((bf16[1,2,256,8192]{2,1,0,3:T(2,128)(2,1)}), bf16[1,2,256,8192]{2,1,0,3:T(2,128)(2,1)}, u32[]{:S(2)}, u32[]{:S(2)}) %all-to-all-start.2) | async-done | bytes 8388640 | tf_op jit(solution)/shard_map/all_to_all | solution.py:196
  421.8 11.9 %copy.206 = bf16[1,2,16,256,512]{4,3,2,1,0:T(8,128)(2,1)} copy(bf16[1,2,16,256,512]{3,4,2,1,0:T(8,128)(2,1)} %bitcast.219) | data formatting | bytes 16777216 | tf_op jit(solution)/shard_map/all_to_all | solution.py:196
  448.7 14.3 %fusion.14 = f32[2,32,128,512]{3,1,2,0:T(8,128)S(1)} fusion(bf16[2,32,128,512]{3,2,1,0:T(8,128)(2,1)} %pad_maximum_fusion.5, bf16[1,2,32,32]{2,3,1,0:T(8,128)(2,1)S(1)} %get-tuple-element.43, bf16[1,2,32,32]{2,3,1,0:T(8,128)(2,1)S(1)} %get-tuple-element.42), kind=kOutput, calls=%fused_computation.35 | convolution fusion | flops 545263616 | bytes 25174016 | tf_op jit(solution)/shard_map/dikyb,iokx->doxyb/dot_general | solution.py:82
  463.0 19.7 %copy.211 = f32[2,32,128,512]{3,2,1,0:T(8,128)} copy(f32[2,32,128,512]{3,1,2,0:T(8,128)S(1)} %fusion.14) | data formatting | bytes 33554432 | tf_op jit(solution)/shard_map/convert_element_type | solution.py:143
  482.7 9.6 fusion.15
  492.3 8.9 copy.212
  509.4 22.4 %reduce.2 = bf16[4096,32]{1,0:T(8,128)(2,1)S(1)} reduce(bf16[4096,1,32]{2,1,0:T(2,128)(2,1)S(1)} %bitcast.229, bf16[]{:T(256)} %broadcast.2052), dimensions={1}, to_apply=%bitcast.198.reduce_sub_computation | reduce | bytes 524290
  533.5 60.3 %all-to-all-done = bf16[2,256,8192]{1,0,2:T(2,128)(2,1)} async-done(((bf16[2,256,8192]{1,0,2:T(2,128)(2,1)}), bf16[2,256,8192]{1,0,2:T(2,128)(2,1)}, u32[]{:S(2)}, u32[]{:S(2)}) %all-to-all-start) | async-done | bytes 8388640 | tf_op jit(solution)/shard_map/all_to_all | solution.py:158
  606.5 11.9 %copy.185 = bf16[2,16,256,512]{3,2,1,0:T(8,128)(2,1)} copy(bf16[2,16,256,512]{2,3,1,0:T(8,128)(2,1)} %bitcast.220) | data formatting | bytes 16777216 | tf_op jit(solution)/shard_map/all_to_all | solution.py:158
  618.4 14.3 %fusion.36 = f32[1,2,32,128,512]{4,2,3,1,0:T(8,128)S(1)} fusion(bf16[2,32,128,512]{3,2,1,0:T(8,128)(2,1)} %bitcast.216, bf16[1,2,32,32]{2,3,0,1:T(8,128)(2,1)S(1)} %get-tuple-element.45, bf16[1,2,32,32]{2,3,0,1:T(8,128)(2,1)S(1)} %get-tuple-element.44), kind=kOutput, calls=%fused_computation.82 | convolution fusion | flops 536887296 | bytes 25174016 | tf_op jit(solution)/shard_map/dixyb,ioxk->dokyb/dot_general | solution.py:82
  643.2 13.8 %fusion.39 = f32[1,2,32,128,512]{4,3,2,1,0:T(8,128)S(1)} fusion(bf16[2,32,128,512]{3,1,2,0:T(8,128)(2,1)} %pad_maximum_fusion, bf16[1,2,128,128]{2,3,0,1:T(8,128)(2,1)S(1)} %get-tuple-element.37, bf16[1,2,128,128]{2,3,0,1:T(8,128)(2,1)S(1)} %get-tuple-element.36), kind=kOutput, calls=%fused_computation.83 | convolution fusion | flops 2147745792 | bytes 25296896 | tf_op jit(solution)/shard_map/dikyb,ioyq->dokqb/dot_general | solution.py:82
  657.0 36.5 %subtract_convert_fusion.5 = (bf16[1,1,32,128,512]{4,3,2,1,0:T(8,128)(2,1)S(1)}, bf16[1,1,32,128,512]{4,3,2,1,0:T(8,128)(2,1)S(1)}) fusion(f32[1,2,32,128,512]{4,3,2,1,0:T(8,128)S(1)} %fusion.39, s32[512]{0:T(512)S(1)} %iota_add_fusion.3, s32[32,128]{1,0:T(8,128)S(1)} %iota_add_fusion.2), kind=kLoop, calls=%fused_computation.79 | loop fusion | flops 46137344 | bytes 25184256 | tf_op jit(solution)/shard_map/convert.49
  693.5 31.1 %copy.190 = bf16[1,1,4096,512]{3,1,0,2:T(2,128)(2,1)S(1)} copy(bf16[1,1,4096,512]{3,2,1,0:T(8,128)(2,1)S(1)} %bitcast.224) | data formatting | bytes 8388608 | tf_op jit(solution)/shard_map/stack | solution.py:78
  724.6 31.1 %copy.191 = bf16[1,1,4096,512]{3,1,0,2:T(2,128)(2,1)S(1)} copy(bf16[1,1,4096,512]{3,2,1,0:T(8,128)(2,1)S(1)} %bitcast.223) | data formatting | bytes 8388608 | tf_op jit(solution)/shard_map/stack | solution.py:78
  755.7 20.3 %pad_maximum_fusion.1 = bf16[1,2,4096,512]{3,1,0,2:T(2,128)(2,1)} fusion(bf16[1,1,4096,512]{3,1,0,2:T(2,128)(2,1)S(1)} %copy.191, bf16[1,1,4096,512]{3,1,0,2:T(2,128)(2,1)S(1)} %copy.190), kind=kLoop, calls=%fused_computation.41 | loop fusion | flops 16777216 | bytes 16777216 | tf_op jit(solution)/shard_map/stack | solution.py:78
  793.8 170.2 %collective-permute-done = bf16[1,16]{1,0:T(2,128)(2,1)S(1)} collective-permute-done((bf16[1,16]{1,0:T(2,128)(2,1)S(1)}, bf16[1,16]{1,0:T(2,128)(2,1)S(1)}, u32[]{:S(2)}, u32[]{:S(2)}) %collective-permute-start) | collective-permute-done | bytes 64 | tf_op jit(solution)/shard_map/ppermute | solution.py:24
  972.9 36.0 %fusion.69 = f32[1,131072]{1,0:T(1,128)} fusion(f32[1,131104]{1,0:T(1,128)S(1)} %convert_element_type.400), kind=kLoop, calls=%fused_computation.105 | loop fusion | flops 4325376 | bytes 17825792 | tf_op jit(solution)/shard_map/div | solution.py:209
  1008.9 15.9 %copy.287 = bf16[1,2,16,256,512]{4,2,1,3,0:T(8,128)(2,1)} copy(bf16[1,2,16,256,512]{4,1,3,2,0:T(2,128)(2,1)} %bitcast.33) | data formatting | bytes 16777216 | tf_op jit(solution)/shard_map/all_to_all | solution.py:179
  1024.7 13.9 %reshape.1466 = bf16[2,256,64,128,1]{3,2,0,1,4:T(8,128)(2,1)} reshape(bf16[1,2,256,16,512]{4,3,1,2,0:T(8,128)(2,1)} %bitcast.221) | data formatting | bytes 16777216 | tf_op jit(solution)/shard_map/reshape.24
  1054.9 16.7 %bitcast_convert_fusion.1 = bf16[2,128,256,64]{2,1,3,0:T(8,128)(2,1)} fusion(bf16[2,256,64,128]{3,2,1,0:T(8,128)(2,1)} %pad_maximum_fusion.2, bf16[1,2,128,128]{2,3,0,1:T(8,128)(2,1)S(1)} %get-tuple-element.37, bf16[1,2,128,128]{2,3,0,1:T(8,128)(2,1)S(1)} %get-tuple-element.36), kind=kOutput, calls=%fused_computation.1 | convolution fusion | flops 2151940096 | bytes 16908288 | tf_op jit(solution)/shard_map/dimjy,ioyq->domjq/dot_general | solution.py:82
  1071.7 12.0 %copy.216 = bf16[2,256,8192]{2,1,0:T(8,128)(2,1)} copy(bf16[2,256,8192]{1,2,0:T(8,128)(2,1)} %bitcast.217) | data formatting | bytes 16777216
  (83 shorter events, 162.4 us)
Async XLA Ops:
  217.6 189.1 %all-to-all-start.2 = ((bf16[1,2,256,8192]{2,1,0,3:T(2,128)(2,1)}), bf16[1,2,256,8192]{2,1,0,3:T(2,128)(2,1)}, u32[]{:S(2)}, u32[]{:S(2)}) async-start(bf16[1,2,256,8192]{2,1,0,3:T(2,128)(2,1)} %copy.204), calls=%async_computation.2 | async-start | bytes 16777216 | tf_op jit(solution)/shard_map/all_to_all | solution.py:196
  406.7 187.1 %all-to-all-start = ((bf16[2,256,8192]{1,0,2:T(2,128)(2,1)}), bf16[2,256,8192]{1,0,2:T(2,128)(2,1)}, u32[]{:S(2)}, u32[]{:S(2)}) async-start(bf16[2,256,8192]{1,0,2:T(2,128)(2,1)} %copy.183), calls=%async_computation | async-start | bytes 16777216 | tf_op jit(solution)/shard_map/all_to_all | solution.py:158
  593.8 182.2 %all-to-all-start.3 = ((bf16[16,2,4096]{2,1,0:T(2,128)(2,1)}), bf16[16,2,4096]{2,1,0:T(2,128)(2,1)S(1)}, u32[]{:S(2)}, u32[]{:S(2)}) async-start(bf16[16,2,4096]{2,1,0:T(2,128)(2,1)} %reshape.1483), calls=%async_computation.3 | async-start | bytes 524288 | tf_op jit(solution)/shard_map/all_to_all | solution.py:198
  776.0 188.0 %copy-start = (bf16[1,131104]{1,0:T(2,128)(2,1)S(1)}, bf16[1,131104]{1,0:T(2,128)(2,1)}, u32[]{:S(2)}) copy-start(bf16[1,131104]{1,0:T(2,128)(2,1)} %custom-call) | copy-start | bytes 786628
  776.0 232.9 %all-to-all-start.1 = ((bf16[1,2,4096,512]{3,1,0,2:T(2,128)(2,1)}), bf16[1,2,4096,512]{3,1,0,2:T(2,128)(2,1)}, u32[]{:S(2)}, u32[]{:S(2)}) async-start(bf16[1,2,4096,512]{3,1,0,2:T(2,128)(2,1)} %pad_maximum_fusion.1), calls=%async_computation.1 | async-start | bytes 16777216 | tf_op jit(solution)/shard_map/all_to_all | solution.py:179
  787.3 176.7 %collective-permute-start = (bf16[1,16]{1,0:T(2,128)(2,1)S(1)}, bf16[1,16]{1,0:T(2,128)(2,1)S(1)}, u32[]{:S(2)}, u32[]{:S(2)}) collective-permute-start(bf16[1,16]{1,0:T(2,128)(2,1)S(1)} %get-tuple-element.33), channel_id=1, source_target_pairs={{0,1},{1,2},{2,3},{3,4},{4,5},{5,6},{6,7},{7,8},{8,9},{9,10},{10,1... | collective-permute-start | bytes 104 | tf_op jit(solution)/shard_map/ppermute | solution.py:24
  789.4 182.7 %collective-permute-start.1 = (bf16[1,16]{1,0:T(2,128)(2,1)S(1)}, bf16[1,16]{1,0:T(2,128)(2,1)S(1)}, u32[]{:S(2)}, u32[]{:S(2)}) collective-permute-start(bf16[1,16]{1,0:T(2,128)(2,1)S(1)} %get-tuple-element.32), channel_id=1, source_target_pairs={{1,0},{2,1},{3,2},{4,3},{5,4},{6,5},{7,6},{8,7},{9,8},{10,9},{11,1... | collective-permute-start | bytes 104 | tf_op jit(solution)/shard_map/ppermute | solution.py:27
  1038.7 5.8 copy-start.1
  1038.7 5.8 copy-start.2
where the time goes:
time: 1100 us; the launch traced here: 1080 us
  waiting for transfers between devices  379 us (34%)
  local copies, waits for them, and re-layouts  325 us (30%)
  other arithmetic  266 us (24%)
  matrix products  82.4 us (7%)
  starting transfers between devices  28.9 us (3%)
    ppermute x1, waiting for transfers between devices, padded_2(): lax.ppermute(lax.slice_in_dim(block, block.shape[dim] - width, None, axis...  170 us
    all_to_all x1, waiting for transfers between devices, on_device(): lax.all_to_all(front_part, 'fft', split_axis=3, concat_axis=2, tiled=True)  149 us
    another operation x11, other arithmetic, rotate(): return jnp.stack([real_part, imag_part], axis=1).astype(jnp.bfloat16)  115 us
    another operation x4, local copies, waits for them, and re-layouts, rotate(): return jnp.stack([real_part, imag_part], axis=1).astype(jnp.bfloat16)  90.7 us
    dot_general x8, matrix products, dft_section(): jnp.einsum(einsum_form, values, dft_table(length, direction), preferred_e...  82.4 us
    another operation x14, other arithmetic  75.7 us
    unnamed x17, local copies, waits for them, and re-layouts  66.2 us
    all_to_all x1, waiting for transfers between devices, on_device(): lax.all_to_all(values, 'fft', split_axis=2, concat_axis=1, tiled=True)  60.3 us
  transfers between devices with their start and end apart: 6, of which 3 were waited for; matrix products, arithmetic and copies ran while one was open for 35% of the time, Pallas kernels for 0%

commit v1 on v0

--- a/solution.py
+++ b/solution.py
@@ -193,7 +193,10 @@
     row_start = device_index * row_local
     trial_total = dm_index.shape[0]
     front_part = chirp_front(spectrum_in, grid_steps, row_start, row_local)
-    moved = lax.all_to_all(front_part, "fft", split_axis=3, concat_axis=2, tiled=True)
+    moved = jnp.concatenate(
+        lax.all_to_all(jnp.stack(jnp.split(front_part, lax.axis_size("fft"), axis=3)), "fft", 0, 0),
+        axis=2,
+    )
     pieces = finish_rows(moved)
     decimated_power = lax.all_to_all(
         detect(pieces).astype(jnp.bfloat16), "fft", split_axis=1, concat_axis=2, tiled=True

time: 1100 us -> 1090 us (level)
  local copies, waits for them, and re-layouts: 325 us -> 303 us
    all_to_all x2 -> x0, local copies, waits for them, and re-layouts: 19.7 us -> none  [on_device(): lax.all_to_all(front_part, 'fft', split_axis=3, concat_axis=2, tiled=True)]
    another operation x4 -> x3, local copies, waits for them, and re-layouts: 90.7 us -> 74.4 us  [rotate(): return jnp.stack([real_part, imag_part], axis=1).astype(jnp.bfloat16)]
    unnamed x2 -> x17, other arithmetic: 22.4 us -> 36.2 us
    reshape x0 -> x1, local copies, waits for them, and re-layouts: none -> 11.9 us  [on_device(): jnp.concatenate(lax.all_to_all(jnp.stack(jnp.split(front_part, lax.axis_s...]
    another operation x11 -> x10, other arithmetic: 115 us -> 108 us  [rotate(): return jnp.stack([real_part, imag_part], axis=1).astype(jnp.bfloat16)]
    unnamed x17 -> x23, local copies, waits for them, and re-layouts: 66.2 us -> 68 us
    another operation x14 -> x15, other arithmetic: 75.7 us -> 76.6 us
where the time goes in v1:
time: 1090 us; the launch traced here: 1080 us
  waiting for transfers between devices  386 us (35%)
  local copies, waits for them, and re-layouts  303 us (28%)
  other arithmetic  274 us (25%)
  matrix products  82.4 us (8%)
  starting transfers between devices  28.9 us (3%)
    ppermute x1, waiting for transfers between devices, padded_2(): lax.ppermute(lax.slice_in_dim(block, block.shape[dim] - width, None, axis...  170 us
    all_to_all x1, waiting for transfers between devices, on_device(): lax.all_to_all(jnp.stack(jnp.split(front_part, lax.axis_size('fft'), axis...  149 us
    another operation x10, other arithmetic, rotate(): return jnp.stack([real_part, imag_part], axis=1).astype(jnp.bfloat16)  108 us
    dot_general x8, matrix products, dft_section(): jnp.einsum(einsum_form, values, dft_table(length, direction), preferred_e...  82.4 us
    another operation x14, other arithmetic  75.7 us
    another operation x3, local copies, waits for them, and re-layouts, rotate(): return jnp.stack([real_part, imag_part], axis=1).astype(jnp.bfloat16)  74.4 us
    unnamed x23, local copies, waits for them, and re-layouts  68 us
    all_to_all x1, waiting for transfers between devices, on_device(): lax.all_to_all(values, 'fft', split_axis=2, concat_axis=1, tiled=True)  67 us
  transfers between devices with their start and end apart: 6, of which 3 were waited for; matrix products, arithmetic and copies ran while one was open for 35% of the time, Pallas kernels for 0%

profile of v1, /device:TPU:16, one launch (start us, length us, event | category | flops | bytes accessed | tf_op | source)
XLA Modules:
  0.0 1076.3 jit_solution(1146254545277586247)
XLA Ops:
  2.5 11.9 %copy.192 = bf16[2,256,8192]{1,2,0:T(8,128)(2,1)} copy(bf16[2,256,8192]{2,1,0:T(8,128)(2,1)} %param.4) | data formatting | bytes 16777216 | tf_op args[1]
  14.4 11.6 %fusion.146 = (f32[1,1,256,64,128]{2,4,3,1,0:T(8,128)}, f32[1,1,256,64,128]{2,4,3,1,0:T(8,128)}) fusion(bf16[1,2,256,64,128]{2,4,3,1,0:T(8,128)(2,1)} %bitcast.276), kind=kLoop, calls=%fused_computation.349 | loop fusion | bytes 33554432 | tf_op jit(solution)/shard_map/slice | solution.py:76
  26.0 9.1 copy.236
  35.0 9.0 copy.237
  44.0 41.0 %fusion.57 = (bf16[1,256,64,128]{3,1,0,2:T(8,128)(2,1)S(1)}, bf16[1,256,64,128]{3,1,0,2:T(8,128)(2,1)S(1)}) fusion(f32[1,1,256,64,128]{4,2,3,1,0:T(8,128)} %copy.237, f32[1,1,256,64,128]{4,2,3,1,0:T(8,128)} %copy.236, f32[64,128]{1,0:T(8,128)S(1)} %fusion.114, s32[64,128]{1,0:T(8,128)S(1)} %iota_add_fusion.1, s32[256]{0:T(256)S(1)} %fusion.139, ...), kind=kLoop, calls=%fused_computation.121 | loop fusion | flops 77594624 | bytes 25233412 | tf_op jit(solution)/shard_map/stack | solution.py:78
  92.1 8.8 fusion.59
  107.2 12.2 %copy.198 = bf16[2,256,64,128]{3,2,0,1:T(8,128)(2,1)} copy(bf16[2,256,64,128]{1,3,2,0:T(8,128)(2,1)} %pad_maximum_fusion.3) | data formatting | bytes 16777216 | tf_op jit(solution)/shard_map/stack | solution.py:78
  125.2 18.3 %copy.281 = f32[2,64,256,128]{3,2,1,0:T(8,128)S(1)} copy(f32[2,64,256,128]{3,1,2,0:T(8,128)S(1)} %fusion.48) | data formatting | bytes 33554432 | tf_op jit(solution)/shard_map/dimjy,iojx->domxy/dot_general | solution.py:82
  143.6 37.2 %subtract_convert_fusion.1 = (bf16[1,1,256,64,128]{4,2,3,1,0:T(8,128)(2,1)}, bf16[1,1,256,64,128]{4,2,3,1,0:T(8,128)(2,1)}) fusion(f32[1,2,256,64,128]{4,2,3,1,0:T(8,128)S(1)} %bitcast.277, s32[64,128]{1,0:T(8,128)S(1)} %iota_add_fusion, s32[256]{0:T(256)S(1)} %fusion.139), kind=kLoop, calls=%fused_computation.100 | loop fusion | flops 46137344 | bytes 25199616 | tf_op jit(solution)/shard_map/convert.9
  216.6 12.7 %copy.282 = bf16[1,2,256,8192]{3,2,1,0:T(8,128)(2,1)} copy(bf16[1,2,256,8192]{3,1,2,0:T(2,128)(2,1)} %bitcast.289) | data formatting | bytes 16777216
  229.3 21.0 %copy.181 = bf16[2,256,8192]{1,0,2:T(2,128)(2,1)} copy(bf16[2,256,8192]{2,1,0:T(8,128)(2,1)} %bitcast.285) | data formatting | bytes 16777216 | tf_op jit(solution)/shard_map/reshape | solution.py:157
  250.3 148.7 %all-to-all-done.2 = bf16[16,1,2,256,512]{3,4,2,1,0:T(8,128)(2,1)} async-done(((bf16[16,1,2,256,512]{3,4,2,1,0:T(8,128)(2,1)}), bf16[16,1,2,256,512]{3,4,2,1,0:T(8,128)(2,1)}, u32[]{:S(2)}, u32[]{:S(2)}) %all-to-all-start.2) | async-done | bytes 8388640 | tf_op jit(solution)/shard_map/all_to_all | solution.py:197
  407.4 11.9 %copy.202 = bf16[1,2,16,256,512]{4,3,2,1,0:T(8,128)(2,1)} copy(bf16[1,2,16,256,512]{3,4,1,0,2:T(8,128)(2,1)} %bitcast.97) | data formatting | bytes 16777216 | tf_op jit(solution)/shard_map/reshape | solution.py:196
  434.3 14.3 %fusion.14 = f32[2,32,128,512]{3,1,2,0:T(8,128)S(1)} fusion(bf16[2,32,128,512]{3,2,1,0:T(8,128)(2,1)} %pad_maximum_fusion.4, bf16[1,2,32,32]{2,3,1,0:T(8,128)(2,1)S(1)} %get-tuple-element.43, bf16[1,2,32,32]{2,3,1,0:T(8,128)(2,1)S(1)} %get-tuple-element.42), kind=kOutput, calls=%fused_computation.65 | convolution fusion | flops 545263616 | bytes 25174016 | tf_op jit(solution)/shard_map/dikyb,iokx->doxyb/dot_general | solution.py:82
  448.6 19.7 %copy.207 = f32[2,32,128,512]{3,2,1,0:T(8,128)} copy(f32[2,32,128,512]{3,1,2,0:T(8,128)S(1)} %fusion.14) | data formatting | bytes 33554432 | tf_op jit(solution)/shard_map/convert_element_type | solution.py:143
  468.2 9.6 fusion.15
  477.8 9.0 copy.208
  495.0 22.4 %reduce.2 = bf16[4096,32]{1,0:T(8,128)(2,1)S(1)} reduce(bf16[4096,1,32]{2,1,0:T(2,128)(2,1)S(1)} %bitcast.290, bf16[]{:T(256)} %broadcast.2052), dimensions={1}, to_apply=%bitcast.230.reduce_sub_computation | reduce | bytes 524290
  519.1 67.0 %all-to-all-done = bf16[2,256,8192]{1,0,2:T(2,128)(2,1)} async-done(((bf16[2,256,8192]{1,0,2:T(2,128)(2,1)}), bf16[2,256,8192]{1,0,2:T(2,128)(2,1)}, u32[]{:S(2)}, u32[]{:S(2)}) %all-to-all-start) | async-done | bytes 8388640 | tf_op jit(solution)/shard_map/all_to_all | solution.py:158
  598.8 11.9 %copy.183 = bf16[2,16,256,512]{3,2,1,0:T(8,128)(2,1)} copy(bf16[2,16,256,512]{2,3,1,0:T(8,128)(2,1)} %bitcast.283) | data formatting | bytes 16777216 | tf_op jit(solution)/shard_map/all_to_all | solution.py:158
  610.7 14.3 %fusion.36 = f32[1,2,32,128,512]{4,2,3,1,0:T(8,128)S(1)} fusion(bf16[2,32,128,512]{3,2,1,0:T(8,128)(2,1)} %bitcast.280, bf16[1,2,32,32]{2,3,0,1:T(8,128)(2,1)S(1)} %copy-done.3, bf16[1,2,32,32]{2,3,0,1:T(8,128)(2,1)S(1)} %get-tuple-element.44), kind=kOutput, calls=%fused_computation.111 | convolution fusion | flops 536887296 | bytes 25174016 | tf_op jit(solution)/shard_map/dixyb,ioxk->dokyb/dot_general | solution.py:82
  635.5 13.8 %fusion.39 = f32[1,2,32,128,512]{4,3,2,1,0:T(8,128)S(1)} fusion(bf16[2,32,128,512]{3,1,2,0:T(8,128)(2,1)} %pad_maximum_fusion, bf16[1,2,128,128]{2,3,0,1:T(8,128)(2,1)S(1)} %get-tuple-element.37, bf16[1,2,128,128]{2,3,0,1:T(8,128)(2,1)S(1)} %get-tuple-element.36), kind=kOutput, calls=%fused_computation.112 | convolution fusion | flops 2147745792 | bytes 25296896 | tf_op jit(solution)/shard_map/dikyb,ioyq->dokqb/dot_general | solution.py:82
  649.4 36.5 %subtract_convert_fusion.5 = (bf16[1,1,32,128,512]{4,3,2,1,0:T(8,128)(2,1)S(1)}, bf16[1,1,32,128,512]{4,3,2,1,0:T(8,128)(2,1)S(1)}) fusion(f32[1,2,32,128,512]{4,3,2,1,0:T(8,128)S(1)} %fusion.39, s32[512]{0:T(512)S(1)} %copy-done.5, s32[32,128]{1,0:T(8,128)S(1)} %copy-done.4), kind=kLoop, calls=%fused_computation.108 | loop fusion | flops 46137344 | bytes 25184256 | tf_op jit(solution)/shard_map/convert.49
  685.9 31.1 %copy.188 = bf16[1,1,4096,512]{3,1,0,2:T(2,128)(2,1)S(1)} copy(bf16[1,1,4096,512]{3,2,1,0:T(8,128)(2,1)S(1)} %bitcast.287) | data formatting | bytes 8388608 | tf_op jit(solution)/shard_map/stack | solution.py:78
  717.0 31.1 %copy.189 = bf16[1,1,4096,512]{3,1,0,2:T(2,128)(2,1)S(1)} copy(bf16[1,1,4096,512]{3,2,1,0:T(8,128)(2,1)S(1)} %bitcast.286) | data formatting | bytes 8388608 | tf_op jit(solution)/shard_map/stack | solution.py:78
  748.1 20.3 %pad_maximum_fusion.1 = bf16[1,2,4096,512]{3,1,0,2:T(2,128)(2,1)} fusion(bf16[1,1,4096,512]{3,1,0,2:T(2,128)(2,1)S(1)} %copy.189, bf16[1,1,4096,512]{3,1,0,2:T(2,128)(2,1)S(1)} %copy.188), kind=kLoop, calls=%fused_computation.71 | loop fusion | flops 16777216 | bytes 16777216 | tf_op jit(solution)/shard_map/stack | solution.py:78
  786.2 170.2 %collective-permute-done = bf16[1,16]{1,0:T(2,128)(2,1)S(1)} collective-permute-done((bf16[1,16]{1,0:T(2,128)(2,1)S(1)}, bf16[1,16]{1,0:T(2,128)(2,1)S(1)}, u32[]{:S(2)}, u32[]{:S(2)}) %collective-permute-start) | collective-permute-done | bytes 64 | tf_op jit(solution)/shard_map/ppermute | solution.py:24
  965.2 36.0 %fusion.84 = f32[1,131072]{1,0:T(1,128)} fusion(f32[1,131104]{1,0:T(1,128)S(1)} %convert_element_type.400), kind=kLoop, calls=%fused_computation.149 | loop fusion | flops 4325376 | bytes 17825792 | tf_op jit(solution)/shard_map/div | solution.py:212
  1001.2 15.9 %copy.283 = bf16[1,2,16,256,512]{4,2,1,3,0:T(8,128)(2,1)} copy(bf16[1,2,16,256,512]{4,1,3,2,0:T(2,128)(2,1)} %bitcast.33) | data formatting | bytes 16777216 | tf_op jit(solution)/shard_map/all_to_all | solution.py:179
  1017.1 13.9 %reshape.1468 = bf16[2,256,64,128,1]{3,2,0,1,4:T(8,128)(2,1)} reshape(bf16[1,2,256,16,512]{4,3,1,2,0:T(8,128)(2,1)} %bitcast.284) | data formatting | bytes 16777216 | tf_op jit(solution)/shard_map/reshape.24
  1047.3 16.7 %bitcast_convert_fusion.1 = bf16[2,128,256,64]{2,1,3,0:T(8,128)(2,1)} fusion(bf16[2,256,64,128]{3,2,1,0:T(8,128)(2,1)} %pad_maximum_fusion.2, bf16[1,2,128,128]{2,3,0,1:T(8,128)(2,1)S(1)} %get-tuple-element.37, bf16[1,2,128,128]{2,3,0,1:T(8,128)(2,1)S(1)} %get-tuple-element.36), kind=kOutput, calls=%fused_computation.31 | convolution fusion | flops 2151940096 | bytes 16908288 | tf_op jit(solution)/shard_map/dimjy,ioyq->domjq/dot_general | solution.py:82
  1064.0 12.0 %copy.212 = bf16[2,256,8192]{2,1,0:T(8,128)(2,1)} copy(bf16[2,256,8192]{1,2,0:T(8,128)(2,1)} %bitcast.281) | data formatting | bytes 16777216
  (102 shorter events, 155.5 us)
Async XLA Ops:
  193.5 2.5 copy-start
  193.5 3.8 copy-start.1
  209.9 189.1 %all-to-all-start.2 = ((bf16[16,1,2,256,512]{3,4,2,1,0:T(8,128)(2,1)}), bf16[16,1,2,256,512]{3,4,2,1,0:T(8,128)(2,1)}, u32[]{:S(2)}, u32[]{:S(2)}) async-start(bf16[16,1,2,256,512]{3,4,2,1,0:T(8,128)(2,1)} %fusion.86), calls=%async_computation.2 | async-start | bytes 16777216 | tf_op jit(solution)/shard_map/all_to_all | solution.py:197
  399.0 187.1 %all-to-all-start = ((bf16[2,256,8192]{1,0,2:T(2,128)(2,1)}), bf16[2,256,8192]{1,0,2:T(2,128)(2,1)}, u32[]{:S(2)}, u32[]{:S(2)}) async-start(bf16[2,256,8192]{1,0,2:T(2,128)(2,1)} %copy.181), calls=%async_computation | async-start | bytes 16777216 | tf_op jit(solution)/shard_map/all_to_all | solution.py:158
  586.1 182.2 %all-to-all-start.3 = ((bf16[16,2,4096]{2,1,0:T(2,128)(2,1)}), bf16[16,2,4096]{2,1,0:T(2,128)(2,1)S(1)}, u32[]{:S(2)}, u32[]{:S(2)}) async-start(bf16[16,2,4096]{2,1,0:T(2,128)(2,1)} %reshape.1485), calls=%async_computation.3 | async-start | bytes 524288 | tf_op jit(solution)/shard_map/all_to_all | solution.py:201
  598.8 11.9 %copy-start.3 = (bf16[1,2,32,32]{2,3,0,1:T(8,128)(2,1)S(1)}, bf16[1,2,32,32]{2,3,0,1:T(8,128)(2,1)}, u32[]{:S(2)}) copy-start(bf16[1,2,32,32]{2,3,0,1:T(8,128)(2,1)} %get-tuple-element.45) | copy-start | bytes 12292
  635.5 13.8 %copy-start.4 = (s32[32,128]{1,0:T(8,128)S(1)}, s32[32,128]{1,0:T(8,128)}, u32[]{:S(2)}) copy-start(s32[32,128]{1,0:T(8,128)} %iota_add_fusion.2) | copy-start | bytes 49156
  635.5 13.8 %copy-start.5 = (s32[512]{0:T(512)S(1)}, s32[512]{0:T(512)}, u32[]{:S(2)}) copy-start(s32[512]{0:T(512)} %iota_add_fusion.3) | copy-start | bytes 6148
  768.4 188.0 %copy-start.2 = (bf16[1,131104]{1,0:T(2,128)(2,1)S(1)}, bf16[1,131104]{1,0:T(2,128)(2,1)}, u32[]{:S(2)}) copy-start(bf16[1,131104]{1,0:T(2,128)(2,1)} %custom-call) | copy-start | bytes 786628
  768.4 232.9 %all-to-all-start.1 = ((bf16[1,2,4096,512]{3,1,0,2:T(2,128)(2,1)}), bf16[1,2,4096,512]{3,1,0,2:T(2,128)(2,1)}, u32[]{:S(2)}, u32[]{:S(2)}) async-start(bf16[1,2,4096,512]{3,1,0,2:T(2,128)(2,1)} %pad_maximum_fusion.1), calls=%async_computation.1 | async-start | bytes 16777216 | tf_op jit(solution)/shard_map/all_to_all | solution.py:179
  779.7 176.7 %collective-permute-start = (bf16[1,16]{1,0:T(2,128)(2,1)S(1)}, bf16[1,16]{1,0:T(2,128)(2,1)S(1)}, u32[]{:S(2)}, u32[]{:S(2)}) collective-permute-start(bf16[1,16]{1,0:T(2,128)(2,1)S(1)} %get-tuple-element.33), channel_id=1, source_target_pairs={{0,1},{1,2},{2,3},{3,4},{4,5},{5,6},{6,7},{7,8},{8,9},{9,10},{10,1... | collective-permute-start | bytes 104 | tf_op jit(solution)/shard_map/ppermute | solution.py:24
  781.7 182.7 %collective-permute-start.1 = (bf16[1,16]{1,0:T(2,128)(2,1)S(1)}, bf16[1,16]{1,0:T(2,128)(2,1)S(1)}, u32[]{:S(2)}, u32[]{:S(2)}) collective-permute-start(bf16[1,16]{1,0:T(2,128)(2,1)S(1)} %get-tuple-element.32), channel_id=1, source_target_pairs={{1,0},{2,1},{3,2},{4,3},{5,4},{6,5},{7,6},{8,7},{9,8},{10,9},{11,1... | collective-permute-start | bytes 104 | tf_op jit(solution)/shard_map/ppermute | solution.py:27
